TPU v7x, 512 devices: a whole 4x4x16 slice. The times are simulated.
512 devices in a mesh: gx: 4 (over y_hi, core), gy: 16 (over z), gz: 8 (over y_lo, x).
Axes of the slice: x: 4, y: 4 (y_hi: 2, y_lo: 2; y = y_hi * 2 + y_lo), z: 16, core: 2. Of those that a mesh axis runs over, the one named last changes fastest.
Arguments:
- heat_level_grid: float32 [256, 1024, 512], P('gz', 'gy', 'gx'), may hold values from -16 to 16, as said below
- interval_first_class: int32 [1], replicated, may hold values from 0 to 95
- interval_beyond_class: int32 [1], replicated, may hold values from 128 to 256
Outputs:
- magnitude: float32 [256, 1024, 512], P('gz', 'gy', 'gx')
- histogram: float32 [256], replicated
- stats: float32 [4], replicated
Inputs may be any that keep to these rules, and one draw needn't show every extreme that they name: `heat_level_grid`: each entry is a rough value times an amplitude that is constant on blocks of 8 x 4 x 4 cells (z, y, x) and varies over a factor of 16 between blocks.
All inputs are finite; a program needn't handle non-finite values.
Results may differ from a plain program's by a relative error of at most 0.0003.
Values sent between devices are 32-bit elements; how exact they have to be, the bound alone decides.
A program may use at most 64 MiB of HBM per device.

v0:
```python
import jax
import jax.numpy as jnp
from jax import lax
from jax.sharding import Mesh
from jax.sharding import PartitionSpec as P

BINS = 256
GX = ("gx_0", "gx_1")
GZ = ("gz_0", "gz_1")
GX_GY_GZ = ("gx_0", "gx_1", "gy", "gz_0", "gz_1")


stencil_coefficients = (0.8, -0.2, 4.0 / 105.0, -1.0 / 280.0)
grad_range = 12.0


def extended_2(block, sides, width):
    for axis, dim in sides:
        count = lax.axis_size(axis)
        forward = [(i, i + 1) for i in range(count - 1)]
        forward.append((count - 1, 0))
        backward = [(target, source) for source, target in forward]
        low = lax.ppermute(
            lax.slice_in_dim(block, block.shape[dim] - width, None, axis=dim), axis, forward
        )
        high = lax.ppermute(lax.slice_in_dim(block, 0, width, axis=dim), axis, backward)
        block = jnp.concatenate([low, block, high], axis=dim)
    return block


def gathered_once(x, axis):
    leaves = jax.tree.leaves(x)
    turns = sorted(range(len(leaves)), key=lambda k: -leaves[k].size)
    width = (1, *leaves[turns[0]].shape)[-1]
    lines = [
        jnp.pad(leaves[k].reshape(-1), (0, -leaves[k].size % width)).reshape(-1, width)
        for k in turns
    ]
    both, at, found = (lax.all_gather(jnp.concatenate(lines), axis), 0, {})
    for k, line in zip(turns, lines):
        piece = both[:, at : at + len(line)].reshape(len(both), -1)
        found[k] = piece[:, : leaves[k].size].reshape(-1, *leaves[k].shape)
        at += len(line)
    numbers = iter(range(len(leaves)))
    return jax.tree.map(lambda _: found[next(numbers)], x)


def merged_by_axis(x, axes, combine):
    for axis in axes:
        pieces = gathered_once(x, axis)
        x = jax.tree.map(lambda part: part[0], pieces)
        for k in range(1, lax.axis_size(axis)):
            x = combine(x, jax.tree.map(lambda part: part[k], pieces))
    return x


def directional_rate(extended, direction_length_count):
    length = extended.shape[direction_length_count] - 8
    running = jnp.zeros(
        extended.shape[:direction_length_count]
        + (length,)
        + extended.shape[direction_length_count + 1 :],
        jnp.float32,
    )
    for offset, coefficient in enumerate(stencil_coefficients, start=1):
        forward_cells = lax.slice_in_dim(
            extended, 4 + offset, 4 + offset + length, axis=direction_length_count
        )
        backward_cells = lax.slice_in_dim(
            extended, 4 - offset, 4 - offset + length, axis=direction_length_count
        )
        running = running + coefficient * (forward_cells - backward_cells)
    return running


def local_counts(low_bin, fraction):
    cell_count = low_bin.shape[0]
    span_cells = min(cell_count, 32768)
    turn_count = cell_count // span_cells
    coarse_rows = BINS // 16
    coarse_ids = jnp.arange(coarse_rows, dtype=jnp.int32)[:, None]
    finer_ids = jnp.arange(16, dtype=jnp.int32)[:, None]

    def one_turn(turn_index, running):
        start = turn_index * span_cells
        low_part = lax.dynamic_slice_in_dim(low_bin, start, span_cells)
        frac_part = lax.dynamic_slice_in_dim(fraction, start, span_cells)
        high_part = low_part + 1
        coarse = jnp.concatenate([low_part // 16, high_part // 16])
        finer = jnp.concatenate([low_part % 16, high_part % 16])
        weight = jnp.concatenate([1.0 - frac_part, frac_part])
        left_side = jnp.where(coarse[None, :] == coarse_ids, weight[None, :], 0.0)
        right_side = (finer[None, :] == finer_ids).astype(jnp.float32)
        product = lax.dot_general(
            left_side,
            right_side,
            (((1,), (1,)), ((), ())),
            precision=lax.Precision.HIGHEST,
            preferred_element_type=jnp.float32,
        )
        return running + product

    running = lax.fori_loop(0, turn_count, one_turn, jnp.zeros((coarse_rows, 16), jnp.float32))
    return running.reshape(BINS)


def combine_all(first, second):
    return (
        first[0] + second[0],
        first[1] + second[1],
        first[2] + second[2],
        jnp.maximum(first[3], second[3]),
        jnp.minimum(first[4], second[4]),
    )


def on_device(heat_level_grid, interval_first_class, interval_beyond_class):
    grad_x = directional_rate(extended_2(heat_level_grid, ((GX, 2),), 4), 2)
    grad_y = directional_rate(extended_2(heat_level_grid, (("gy", 1),), 4), 1)
    grad_z = directional_rate(extended_2(heat_level_grid, ((GZ, 0),), 4), 0)
    slope_norm_square = grad_z * grad_z + grad_y * grad_y + grad_x * grad_x
    magnitude = jnp.sqrt(slope_norm_square + 1.0) - 1.0
    position = jnp.clip(magnitude * (BINS / grad_range), 0.5, BINS - 0.5)
    low_bin = jnp.minimum(jnp.floor(position - 0.5), BINS - 2).astype(jnp.int32)
    fraction = position - 0.5 - low_bin.astype(jnp.float32)
    counts = local_counts(low_bin.reshape(-1), fraction.reshape(-1))
    lower_edge = interval_first_class[0]
    upper_edge = interval_beyond_class[0]
    high_bin = low_bin + 1
    inside_low = (low_bin >= lower_edge) & (low_bin < upper_edge)
    inside_high = (high_bin >= lower_edge) & (high_bin < upper_edge)
    weight = jnp.where(inside_low, 1.0 - fraction, 0.0) + jnp.where(inside_high, fraction, 0.0)
    lowest = jnp.min(magnitude + grad_range * (1.0 - weight))
    highest = jnp.max(weight * magnitude)
    weighted_sum = jnp.sum(weight * magnitude)
    weighted_count = jnp.sum(weight)
    counts, weighted_sum, weighted_count, highest, lowest = merged_by_axis(
        (counts, weighted_sum, weighted_count, highest, lowest), GX_GY_GZ, combine_all
    )
    total_cells = (
        heat_level_grid.shape[0]
        * heat_level_grid.shape[1]
        * heat_level_grid.shape[2]
        * lax.axis_size(GX)
        * lax.axis_size("gy")
        * lax.axis_size(GZ)
    )
    histogram = counts * (BINS / total_cells)
    stats = jnp.stack([lowest, highest, weighted_sum / total_cells, weighted_count / total_cells])
    return (magnitude, histogram, stats)


def solution(mesh):
    finer = Mesh(
        mesh.devices.reshape(2, 2, mesh.shape["gy"], 2, 4), ("gx_0", "gx_1", "gy", "gz_0", "gz_1")
    )
    return jax.shard_map(
        on_device,
        mesh=finer,
        in_specs=(P(GZ, "gy", GX), P(), P()),
        out_specs=(P(GZ, "gy", GX), P(), P()),
        check_vma=False,
    )
```

profile of v0, /device:TPU:24, one launch (start us, length us, event | category | flops | bytes accessed | tf_op | source)
XLA Modules:
  0.0 224.6 jit_solution(5636302203498421307)
XLA Ops:
  0.6 1.6 fusion.69
  2.3 3.4 %collective-permute-start.1 = (f32[4,64,128]{2,1,0:T(8,128)}, f32[4,64,128]{2,1,0:T(8,128)S(1)}, u32[]{:S(2)}, u32[]{:S(2)}) collective-permute-start(f32[4,64,128]{2,1,0:T(8,128)} %get-tuple-element.248), channel_id=1, source_target_pairs={{0,1},{1,2},{2,3},{3,4},{4,5},{5,6},{6,7},{7,0},{8,9},{9,10},{10,1... | collective-permute-start | bytes 393224 | tf_op jit(solution)/shard_map/ppermute | solution.py:23
  5.7 4.6 %collective-permute-start = (f32[4,64,128]{2,1,0:T(8,128)S(1)}, f32[4,64,128]{2,1,0:T(8,128)S(1)}, u32[]{:S(2)}, u32[]{:S(2)}) collective-permute-start(f32[4,64,128]{2,1,0:T(8,128)S(1)} %get-tuple-element.247), channel_id=1, source_target_pairs={{1,0},{2,1},{3,2},{4,3},{5,4},{6,5},{7,6},{0,7},{9,8},{10,9},{11,1... | collective-permute-start | bytes 393224 | tf_op jit(solution)/shard_map/ppermute | solution.py:26
  10.2 1.9 fusion.71
  12.2 1.0 copy.32
  13.2 1.9 collective-permute-start.5
  15.5 5.1 %collective-permute-start.4 = (f32[32,64,4]{1,0,2:T(8,128)S(1)}, f32[32,64,4]{1,0,2:T(8,128)}, u32[]{:S(2)}, u32[]{:S(2)}) collective-permute-start(f32[32,64,4]{1,0,2:T(8,128)S(1)} %copy.31), channel_id=1, source_target_pairs={{128,0},{256,128},{384,256},{0,384},{129,1},{257,129},{385,257},{1... | collective-permute-start | bytes 98312 | tf_op jit(solution)/shard_map/ppermute | solution.py:26
  20.6 0.7 fusion.70
  21.3 11.4 %collective-permute-start.2 = (f32[32,4,128]{2,1,0:T(4,128)}, f32[32,4,128]{2,1,0:T(4,128)}, u32[]{:S(2)}, u32[]{:S(2)}) collective-permute-start(f32[32,4,128]{2,1,0:T(4,128)} %get-tuple-element.252), channel_id=1, source_target_pairs={{8,0},{16,8},{24,16},{32,24},{40,32},{48,40},{56,48},{64,56},{72,6... | collective-permute-start | bytes 196616 | tf_op jit(solution)/shard_map/ppermute | solution.py:26
  34.0 1.9 collective-permute-start.3
  36.4 1.2 copy.8
  38.1 0.9 constant_dynamic-update-slice_fusion.4
  38.9 2.8 %collective-permute-done.3 = f32[32,4,128]{2,1,0:T(4,128)} collective-permute-done((f32[32,4,128]{2,1,0:T(4,128)}, f32[32,4,128]{2,1,0:T(4,128)}, u32[]{:S(2)}, u32[]{:S(2)}) %collective-permute-start.3) | collective-permute-done | bytes 65568 | tf_op jit(solution)/shard_map/ppermute | solution.py:23
  41.7 6.2 %add_reduce_fusion = (f32[]{:T(128)}, f32[]{:T(128)}, f32[]{:T(128)}, f32[]{:T(128)}, f32[32,64,128]{2,1,0:T(8,128)S(1)}) fusion(s32[]{:T(128)} %bitcast.122, s32[]{:T(128)} %bitcast.121, f32[32,64,128]{2,1,0:T(8,128)S(1)} %copy-done, f32[32,64,4]{2,1,0:T(8,128)S(1)} %copy.10, f32[32,64,4]{2,1,0:T(8,128)S(1)} %copy.8, ...), kind=kLoop, calls=%fused_computation.103 | loop fusion | flops 20709376 | bytes 14811160 | tf_op jit(solution)/shard_map/reduce_min | solution.py:133
  47.9 1.4 convert_subtract_fusion
  49.3 43.6 %while.18 = (s32[]{:T(128)}, f32[16,16]{1,0:T(8,128)S(1)}, s32[262144]{0:T(1024)S(1)}, f32[262144]{0:T(1024)}, s32[]{:T(128)}, /*index=5*/s32[]{:T(128)}, s32[]{:T(128)}, s32[]{:T(128)}) while((s32[]{:T(128)}, f32[16,16]{1,0:T(8,128)S(1)}, s32[262144]{0:T(1024)S(1)}, f32[262144]{0:T(1024)}, s32[]{:T(128)}, ...), condition=%wide.region_1.2_spmd.clone.clone, body=%wide.region_0.1_spmd.clone.clone.sunk | while | flops 206176768 | bytes 5703833 | solution.py:103
  50.2 0.9 broadcast_subtract_fusion.2
  51.2 3.6 %fusion.106 = f32[16,16]{1,0:T(8,128)S(1)} fusion(f32[65536]{0:T(1024)S(1)} %pad_maximum_fusion.6, s32[65536]{0:T(1024)S(1)} %get-tuple-element.425, f32[16,16]{1,0:T(8,128)S(1)} %get-tuple-element.436, pred[]{:T(512)S(6)} %compare.49, pred[16,65536]{1,0:T(8,128)(4,1)S(1)} %iota_compare_fusion.11), kind=kOutput, calls=%fused_computation.9.clone.3 | convolution fusion | flops 203424256 | bytes 1574913 | tf_op jit(solution)/shard_map/while/body/eval_jaxpr/dot_general | solution.py:94
  55.7 0.9 broadcast_subtract_fusion.2
  56.6 3.6 %fusion.106 = f32[16,16]{1,0:T(8,128)S(1)} fusion(f32[65536]{0:T(1024)S(1)} %pad_maximum_fusion.6, s32[65536]{0:T(1024)S(1)} %get-tuple-element.425, f32[16,16]{1,0:T(8,128)S(1)} %get-tuple-element.436, pred[]{:T(512)S(6)} %compare.49, pred[16,65536]{1,0:T(8,128)(4,1)S(1)} %iota_compare_fusion.11), kind=kOutput, calls=%fused_computation.9.clone.3 | convolution fusion | flops 203424256 | bytes 1574913 | tf_op jit(solution)/shard_map/while/body/eval_jaxpr/dot_general | solution.py:94
  61.1 0.9 broadcast_subtract_fusion.2
  62.1 3.6 %fusion.106 = f32[16,16]{1,0:T(8,128)S(1)} fusion(f32[65536]{0:T(1024)S(1)} %pad_maximum_fusion.6, s32[65536]{0:T(1024)S(1)} %get-tuple-element.425, f32[16,16]{1,0:T(8,128)S(1)} %get-tuple-element.436, pred[]{:T(512)S(6)} %compare.49, pred[16,65536]{1,0:T(8,128)(4,1)S(1)} %iota_compare_fusion.11), kind=kOutput, calls=%fused_computation.9.clone.3 | convolution fusion | flops 203424256 | bytes 1574913 | tf_op jit(solution)/shard_map/while/body/eval_jaxpr/dot_general | solution.py:94
  66.6 0.9 broadcast_subtract_fusion.2
  67.5 3.6 %fusion.106 = f32[16,16]{1,0:T(8,128)S(1)} fusion(f32[65536]{0:T(1024)S(1)} %pad_maximum_fusion.6, s32[65536]{0:T(1024)S(1)} %get-tuple-element.425, f32[16,16]{1,0:T(8,128)S(1)} %get-tuple-element.436, pred[]{:T(512)S(6)} %compare.49, pred[16,65536]{1,0:T(8,128)(4,1)S(1)} %iota_compare_fusion.11), kind=kOutput, calls=%fused_computation.9.clone.3 | convolution fusion | flops 203424256 | bytes 1574913 | tf_op jit(solution)/shard_map/while/body/eval_jaxpr/dot_general | solution.py:94
  72.0 0.9 broadcast_subtract_fusion.2
  73.0 3.6 %fusion.106 = f32[16,16]{1,0:T(8,128)S(1)} fusion(f32[65536]{0:T(1024)S(1)} %pad_maximum_fusion.6, s32[65536]{0:T(1024)S(1)} %get-tuple-element.425, f32[16,16]{1,0:T(8,128)S(1)} %get-tuple-element.436, pred[]{:T(512)S(6)} %compare.49, pred[16,65536]{1,0:T(8,128)(4,1)S(1)} %iota_compare_fusion.11), kind=kOutput, calls=%fused_computation.9.clone.3 | convolution fusion | flops 203424256 | bytes 1574913 | tf_op jit(solution)/shard_map/while/body/eval_jaxpr/dot_general | solution.py:94
  77.5 0.9 broadcast_subtract_fusion.2
  78.4 3.6 %fusion.106 = f32[16,16]{1,0:T(8,128)S(1)} fusion(f32[65536]{0:T(1024)S(1)} %pad_maximum_fusion.6, s32[65536]{0:T(1024)S(1)} %get-tuple-element.425, f32[16,16]{1,0:T(8,128)S(1)} %get-tuple-element.436, pred[]{:T(512)S(6)} %compare.49, pred[16,65536]{1,0:T(8,128)(4,1)S(1)} %iota_compare_fusion.11), kind=kOutput, calls=%fused_computation.9.clone.3 | convolution fusion | flops 203424256 | bytes 1574913 | tf_op jit(solution)/shard_map/while/body/eval_jaxpr/dot_general | solution.py:94
  82.9 0.9 broadcast_subtract_fusion.2
  83.9 3.6 %fusion.106 = f32[16,16]{1,0:T(8,128)S(1)} fusion(f32[65536]{0:T(1024)S(1)} %pad_maximum_fusion.6, s32[65536]{0:T(1024)S(1)} %get-tuple-element.425, f32[16,16]{1,0:T(8,128)S(1)} %get-tuple-element.436, pred[]{:T(512)S(6)} %compare.49, pred[16,65536]{1,0:T(8,128)(4,1)S(1)} %iota_compare_fusion.11), kind=kOutput, calls=%fused_computation.9.clone.3 | convolution fusion | flops 203424256 | bytes 1574913 | tf_op jit(solution)/shard_map/while/body/eval_jaxpr/dot_general | solution.py:94
  88.4 0.9 broadcast_subtract_fusion.2
  89.3 3.6 %fusion.106 = f32[16,16]{1,0:T(8,128)S(1)} fusion(f32[65536]{0:T(1024)S(1)} %pad_maximum_fusion.6, s32[65536]{0:T(1024)S(1)} %get-tuple-element.425, f32[16,16]{1,0:T(8,128)S(1)} %get-tuple-element.436, pred[]{:T(512)S(6)} %compare.49, pred[16,65536]{1,0:T(8,128)(4,1)S(1)} %iota_compare_fusion.11), kind=kOutput, calls=%fused_computation.9.clone.3 | convolution fusion | flops 203424256 | bytes 1574913 | tf_op jit(solution)/shard_map/while/body/eval_jaxpr/dot_general | solution.py:94
  93.0 0.6 pad.64
  93.6 0.6 pad.61
  94.8 0.7 pad.63
  95.5 5.9 %all-gather.5 = f32[2,5,256]{2,1,0:T(8,128)S(1)} all-gather(f32[1,5,256]{2,1,0:T(8,128)S(1)} %bitcast.128), channel_id=2, replica_groups=mesh['gx_0'=2,'gx_1'=2,'gy'=16,'gz_0'=2,'gz_1'=4] {'gx_0'}, dimensions={0}, use_global_device_ids=true | all-gather | bytes 15360 | tf_op jit(solution)/shard_map/all_gather | solution.py:39
  108.8 1.8 all-gather.6
  118.0 27.0 %all-gather.7 = f32[16,5,256]{2,1,0:T(8,128)S(1)} all-gather(f32[1,5,256]{2,1,0:T(8,128)S(1)} %bitcast.130), channel_id=4, replica_groups=mesh['gx_0'=2,'gx_1'=2,'gy'=16,'gz_0'=2,'gz_1'=4] {'gy'}, dimensions={0}, use_global_device_ids=true | all-gather | bytes 87040 | tf_op jit(solution)/shard_map/all_gather | solution.py:39
  145.2 0.6 fusion.75
  155.8 0.6 fusion.76
  166.3 0.6 fusion.77
  176.9 0.6 fusion.78
  187.5 4.4 %all-gather.8 = f32[2,5,256]{2,1,0:T(8,128)S(1)} all-gather(f32[1,5,256]{2,1,0:T(8,128)S(1)} %bitcast.131), channel_id=5, replica_groups=mesh['gx_0'=2,'gx_1'=2,'gy'=16,'gz_0'=2,'gz_1'=4] {'gz_0'}, dimensions={0}, use_global_device_ids=true | all-gather | bytes 15360 | tf_op jit(solution)/shard_map/all_gather | solution.py:39
  199.3 11.9 %all-gather.9 = f32[4,5,256]{2,1,0:T(8,128)S(1)} all-gather(f32[1,5,256]{2,1,0:T(8,128)S(1)} %bitcast.132), channel_id=6, replica_groups=mesh['gx_0'=2,'gx_1'=2,'gy'=16,'gz_0'=2,'gz_1'=4] {'gz_1'}, dimensions={0}, use_global_device_ids=true | all-gather | bytes 25600 | tf_op jit(solution)/shard_map/all_gather | solution.py:39
  212.4 0.6 fusion.82
  213.0 0.6 fusion.83
  213.6 0.6 fusion.84
  224.0 0.6 pad_maximum_fusion.4
  (119 shorter events, 16.6 us)
Async XLA Ops:
  2.3 35.3 %collective-permute-start.1 = (f32[4,64,128]{2,1,0:T(8,128)}, f32[4,64,128]{2,1,0:T(8,128)S(1)}, u32[]{:S(2)}, u32[]{:S(2)}) collective-permute-start(f32[4,64,128]{2,1,0:T(8,128)} %get-tuple-element.248), channel_id=1, source_target_pairs={{0,1},{1,2},{2,3},{3,4},{4,5},{5,6},{6,7},{7,0},{8,9},{9,10},{10,1... | collective-permute-start | bytes 393224 | tf_op jit(solution)/shard_map/ppermute | solution.py:23
  5.7 32.3 %collective-permute-start = (f32[4,64,128]{2,1,0:T(8,128)S(1)}, f32[4,64,128]{2,1,0:T(8,128)S(1)}, u32[]{:S(2)}, u32[]{:S(2)}) collective-permute-start(f32[4,64,128]{2,1,0:T(8,128)S(1)} %get-tuple-element.247), channel_id=1, source_target_pairs={{1,0},{2,1},{3,2},{4,3},{5,4},{6,5},{7,6},{0,7},{9,8},{10,9},{11,1... | collective-permute-start | bytes 393224 | tf_op jit(solution)/shard_map/ppermute | solution.py:26
  12.2 8.5 %copy-start = (f32[32,64,128]{2,1,0:T(8,128)S(1)}, f32[32,64,128]{2,1,0:T(8,128)}, u32[]{:S(2)}) copy-start(f32[32,64,128]{2,1,0:T(8,128)} %param.5) | copy-start | bytes 3145732
  13.2 20.8 %collective-permute-start.5 = (f32[32,64,4]{1,0,2:T(8,128)}, f32[32,64,4]{1,0,2:T(8,128)S(1)}, u32[]{:S(2)}, u32[]{:S(2)}) collective-permute-start(f32[32,64,4]{1,0,2:T(8,128)} %copy.32), channel_id=1, source_target_pairs={{0,128},{128,256},{256,384},{384,0},{1,129},{129,257},{257,385},{3... | collective-permute-start | bytes 98312 | tf_op jit(solution)/shard_map/ppermute | solution.py:23
  15.5 20.9 %collective-permute-start.4 = (f32[32,64,4]{1,0,2:T(8,128)S(1)}, f32[32,64,4]{1,0,2:T(8,128)}, u32[]{:S(2)}, u32[]{:S(2)}) collective-permute-start(f32[32,64,4]{1,0,2:T(8,128)S(1)} %copy.31), channel_id=1, source_target_pairs={{128,0},{256,128},{384,256},{0,384},{129,1},{257,129},{385,257},{1... | collective-permute-start | bytes 98312 | tf_op jit(solution)/shard_map/ppermute | solution.py:26
  21.3 16.7 %collective-permute-start.2 = (f32[32,4,128]{2,1,0:T(4,128)}, f32[32,4,128]{2,1,0:T(4,128)}, u32[]{:S(2)}, u32[]{:S(2)}) collective-permute-start(f32[32,4,128]{2,1,0:T(4,128)} %get-tuple-element.252), channel_id=1, source_target_pairs={{8,0},{16,8},{24,16},{32,24},{40,32},{48,40},{56,48},{64,56},{72,6... | collective-permute-start | bytes 196616 | tf_op jit(solution)/shard_map/ppermute | solution.py:26
  34.0 7.7 %collective-permute-start.3 = (f32[32,4,128]{2,1,0:T(4,128)}, f32[32,4,128]{2,1,0:T(4,128)}, u32[]{:S(2)}, u32[]{:S(2)}) collective-permute-start(f32[32,4,128]{2,1,0:T(4,128)} %get-tuple-element.253), channel_id=1, source_target_pairs={{0,8},{8,16},{16,24},{24,32},{32,40},{40,48},{48,56},{56,64},{64,7... | collective-permute-start | bytes 196616 | tf_op jit(solution)/shard_map/ppermute | solution.py:23
  47.9 1.4 copy-start.1
where the time goes:
time: 226 us; the launch traced here: 225 us
  between operations  67.5 us (30%)
  blocking collectives  51 us (23%)
  matrix products  28.5 us (13%)
  starting transfers between devices  28.3 us (13%)
  other arithmetic  23.3 us (10%)
  local copies, waits for them, and re-layouts  22.6 us (10%)
  waiting for transfers between devices  2.81 us (1%)
    all_gather x5, blocking collectives, gathered_once(): both, at, found = (lax.all_gather(jnp.concatenate(lines), axis), 0, {})  51 us
    dot_general x8, matrix products, one_turn(): lax.dot_general(left_side, right_side, (((1,), (1,)), ((), ())), precisio...  28.5 us
    ppermute x3, starting transfers between devices, extended_2(): lax.ppermute(lax.slice_in_dim(block, 0, width, axis=dim), axis, backward)  21.1 us
    slice x20, local copies, waits for them, and re-layouts, merged_by_axis(): x = combine(x, jax.tree.map(lambda part: part[k], pieces))  11.2 us
    sub x8, other arithmetic, one_turn(): weight = jnp.concatenate([1.0 - frac_part, frac_part])  7.43 us
    ppermute x3, starting transfers between devices, extended_2(): lax.ppermute(lax.slice_in_dim(block, block.shape[dim] - width, None, axis...  7.22 us
    reduce_min x1, other arithmetic, on_device(): lowest = jnp.min(magnitude + grad_range * (1.0 - weight))  6.22 us
  transfers between devices with their start and end apart: 6, of which 1 were waited for; matrix products, arithmetic and copies ran while one was open for 3% of the time, Pallas kernels for 0%

commit v1 on v0

v1 whole, which is shorter than its diff:
```python
import jax
import jax.numpy as jnp
from jax import lax
from jax.experimental import pallas as pl
from jax.experimental.pallas import tpu as pltpu
from jax.sharding import PartitionSpec as P

BINS = 256
RANGE = 12.0
COEF = (0.8, -0.2, 4.0 / 105.0, -1.0 / 280.0)
FINE = 11
COARSE = 24
COLS = FINE + 1
MESH = pl.DeviceIdType.MESH
BF = jnp.bfloat16
F32 = jnp.float32


def iota(shape, dim):
    return lax.broadcasted_iota(jnp.int32, shape, dim)


def kernel(nx, ny, nz, cells, first_ref, beyond_ref, x_ref, mag_ref, hist_ref, stat_ref,
           xe, xp, xl, xr, corr, mag, acc, own, plane, line,
           in_sem, out_sem, halo_send, halo_recv, plane_send, plane_recv, line_send, line_recv):
    gx, gy, gz = lax.axis_index("gx"), lax.axis_index("gy"), lax.axis_index("gz")
    zs, ys, lanes = x_ref.shape
    tiles = ys // 8

    load = pltpu.make_async_copy(x_ref, xe.at[pl.ds(4, zs), pl.ds(8, ys), :], in_sem)
    load.start()

    plane_peers = [
        {"gx": lax.rem(gx + dx, nx), "gz": lax.rem(gz + dz, nz)}
        for dx in range(nx) for dz in range(nz) if dx or dz
    ]
    line_peers = [{"gy": lax.rem(gy + d, ny)} for d in range(1, ny)]
    barrier = pltpu.get_barrier_semaphore()
    for peer in plane_peers + line_peers:
        pl.semaphore_signal(barrier, inc=1, device_id=peer, device_id_type=MESH)
    load.wait()

    lane = iota((8, lanes), 1)
    for_group = lane // 8
    part = lane % 8

    def pack(p, carry):
        packed = jnp.zeros((8, lanes), F32)
        for g in range(16):
            tile = xe[4 + 2 * p + g // 8, pl.ds(8 + 8 * (g % 8), 8), :]
            packed = jnp.where(for_group == g, pltpu.roll(tile, (4 + 8 * g) % lanes, 1), packed)
        xp[p] = packed
        return carry

    lax.fori_loop(0, zs // 2, pack, 0)
    acc[...] = jnp.zeros_like(acc)
    pl.semaphore_wait(barrier, len(plane_peers) + len(line_peers))

    def send(i, src, dst, peer):
        copy = pltpu.make_async_remote_copy(
            src_ref=src, dst_ref=dst, send_sem=halo_send.at[i], recv_sem=halo_recv.at[i],
            device_id=peer, device_id_type=MESH)
        copy.start()
        return copy

    up = {"gz": lax.rem(gz + 1, nz)}
    down = {"gz": lax.rem(gz + nz - 1, nz)}
    north = {"gy": lax.rem(gy + 1, ny)}
    south = {"gy": lax.rem(gy + ny - 1, ny)}
    east = {"gx": lax.rem(gx + 1, nx)}
    west = {"gx": lax.rem(gx + nx - 1, nx)}
    mid_y = pl.ds(8, ys)
    mid_z = pl.ds(4, zs)
    halos = [
        send(0, xe.at[pl.ds(zs, 4), mid_y, :], xe.at[pl.ds(0, 4), mid_y, :], up),
        send(1, xe.at[pl.ds(4, 4), mid_y, :], xe.at[pl.ds(zs + 4, 4), mid_y, :], down),
        send(2, xe.at[mid_z, pl.ds(ys, 8), :], xe.at[mid_z, pl.ds(0, 8), :], north),
        send(3, xe.at[mid_z, pl.ds(8, 8), :], xe.at[mid_z, pl.ds(ys + 8, 8), :], south),
        send(4, xp, xl, east),
        send(5, xp, xr, west),
    ]
    for copy in halos:
        copy.wait()

    def correct(p, carry):
        e = jnp.where(part < 4, xl[p], xr[p]) - xp[p]
        high = jnp.where(part >= 4, e, 0.0)
        low = jnp.where(part < 4, e, 0.0)
        ahead = jnp.zeros((8, lanes), F32)
        behind = jnp.zeros((8, lanes), F32)
        for k, c in enumerate(COEF, start=1):
            ahead = ahead + c * pltpu.roll(high, lanes - k, 1)
            behind = behind + c * pltpu.roll(low, k, 1)
        corr[p] = jnp.where(part < 4, ahead, -behind)
        return carry

    lax.fori_loop(0, zs // 2, correct, 0)

    lower = first_ref[0].astype(F32)
    upper = beyond_ref[0].astype(F32)
    edge = (lane < 4) | (lane >= lanes - 4)
    half = jnp.where(iota((16, lanes), 0) < 8, 0.0, 1.0).astype(BF)
    one = jnp.ones((16, lanes), BF)
    zero = jnp.zeros((16, lanes), BF)

    def twice(v):
        return jnp.concatenate([v, v], axis=0).astype(BF)

    def planes(p, carry):
        total, most, least = carry
        for sub in range(2):
            z = 2 * p + sub
            left, right = [], []
            for t in range(tiles):
                row = 8 + 8 * t
                tile = xe[4 + z, pl.ds(row, 8), :]
                rz = jnp.zeros((8, lanes), F32)
                ry = jnp.zeros((8, lanes), F32)
                rx = jnp.where(edge, pltpu.roll(corr[p], (lanes - 8 * (8 * sub + t) - 4) % lanes, 1), 0.0)
                for k, c in enumerate(COEF, start=1):
                    rz = rz + c * (xe[4 + z + k, pl.ds(row, 8), :] - xe[4 + z - k, pl.ds(row, 8), :])
                    ry = ry + c * (xe[4 + z, pl.ds(row + k, 8), :] - xe[4 + z, pl.ds(row - k, 8), :])
                    rx = rx + c * (pltpu.roll(tile, lanes - k, 1) - pltpu.roll(tile, k, 1))
                m = jnp.sqrt(rz * rz + ry * ry + rx * rx + 1.0) - 1.0
                mag[z, pl.ds(8 * t, 8), :] = m
                position = jnp.clip(m * (BINS / RANGE), 0.5, BINS - 0.5) - 0.5
                low = jnp.minimum(jnp.floor(position), BINS - 2.0)
                frac = position - low
                weight = jnp.where((low >= lower) & (low < upper), 1.0 - frac, 0.0) + jnp.where(
                    (low + 1.0 >= lower) & (low + 1.0 < upper), frac, 0.0)
                wm = weight * m
                total = total + wm
                most = jnp.maximum(most, wm)
                least = jnp.minimum(least, m + RANGE * (1.0 - weight))
                coarse = jnp.floor((low + 0.5) * (1.0 / FINE))
                fine = low - FINE * coarse
                big = jnp.floor(frac * 256.0 + 0.5) * (1.0 / 256.0)
                c2 = twice(coarse) - half
                f2 = twice(fine) - half
                th, tl = twice(big), twice(frac - big)
                sh, sl = one - th, zero - tl
                left.append(jnp.concatenate(
                    [jnp.where(c2 == 2.0 * i, one, zero) for i in range(COARSE // 2)], axis=0))
                his, los = [], []
                for i in range(COLS // 2):
                    here, before = f2 == 2.0 * i, f2 == 2.0 * i - 1.0
                    his.append(jnp.where(here, sh, jnp.where(before, th, zero)))
                    los.append(jnp.where(here, sl, jnp.where(before, tl, zero)))
                right.append(jnp.concatenate(his + los, axis=0))
            acc[...] += lax.dot_general(
                jnp.concatenate(left, axis=1), jnp.concatenate(right, axis=1),
                (((1,), (1,)), ((), ())), preferred_element_type=F32)
        return total, most, least

    start = jnp.zeros((8, lanes), F32)
    total, most, least = lax.fori_loop(0, zs // 2, planes, (start, start - jnp.inf, start + jnp.inf))

    store = pltpu.make_async_copy(mag, mag_ref, out_sem)
    store.start()

    rows, cols = 8 * COARSE, 16 * COLS
    prod = jnp.where(iota((rows, cols), 0) % 8 == iota((rows, cols), 1) % 8, acc[...], 0.0)
    table = jnp.sum(prod.reshape(COARSE, 8, cols), axis=1)
    col = (iota((cols, BINS), 0) // 8) % COLS
    bin_ = iota((cols, BINS), 1)
    same = jnp.where(col == bin_ % FINE, 1.0, 0.0)
    over = jnp.where((col == FINE) & (bin_ % FINE == 0), 1.0, 0.0)
    crow = iota((COARSE, BINS), 0)
    cbin = iota((COARSE, BINS), 1) // FINE

    def spread(pick):
        return lax.dot_general(table, pick, (((1,), (0,)), ((), ())), precision=lax.Precision.HIGHEST,
                               preferred_element_type=F32)

    counts = jnp.sum(jnp.where(crow == cbin, spread(same), 0.0) + jnp.where(crow + 1 == cbin, spread(over), 0.0),
                     axis=0, keepdims=True)
    r4, l4 = iota((4, 128), 0), iota((4, 128), 1)
    mine = jnp.where(r4 == 0, counts[:, :128], jnp.where(r4 == 1, counts[:, 128:], 0.0))
    mine = jnp.where((r4 == 2) & (l4 == 0), jnp.sum(total), mine)
    mine = jnp.where((r4 == 2) & (l4 == 1), jnp.max(most), mine)
    mine = jnp.where((r4 == 2) & (l4 == 2), -jnp.min(least), mine)
    is_max = (r4 == 2) & (l4 >= 1)

    def exchange(value, buffer, place, peers, send_sem, recv_sem):
        own[...] = value
        buffer[place] = value
        copies = []
        for i, peer in enumerate(peers):
            copy = pltpu.make_async_remote_copy(
                src_ref=own, dst_ref=buffer.at[place], send_sem=send_sem.at[i], recv_sem=recv_sem.at[i],
                device_id=peer, device_id_type=MESH)
            copy.start()
            copies.append(copy)
        for copy in copies:
            copy.wait()
        added, top = buffer[0], buffer[0]
        for i in range(1, buffer.shape[0]):
            added = added + buffer[i]
            top = jnp.maximum(top, buffer[i])
        return jnp.where(is_max, top, added)

    mine = exchange(mine, plane, gx * nz + gz, plane_peers, plane_send, plane_recv)
    mine = exchange(mine, line, gy, line_peers, line_send, line_recv)

    bins = l4 + 128 * r4
    in_window = (r4 < 2) & (bins >= first_ref[0]) & (bins < beyond_ref[0])
    count = jnp.sum(jnp.where(in_window, mine, 0.0))

    def lane_of(i):
        return jnp.sum(jnp.where((r4 == 2) & (l4 == i), mine, 0.0))

    hist_ref[...] = (mine * (BINS / cells))[:2]
    lo, hi, s = -lane_of(2), lane_of(1), lane_of(0) / cells
    l1 = iota((1, 128), 1)
    stat_ref[...] = jnp.where(l1 == 0, lo, jnp.where(l1 == 1, hi, jnp.where(l1 == 2, s, count / cells)))
    store.wait()


def solution(mesh):
    nx, ny, nz = mesh.shape["gx"], mesh.shape["gy"], mesh.shape["gz"]

    def on_device(x, first, beyond):
        zs, ys, xs = x.shape
        cells = float(zs * ys * xs * nx * ny * nz)
        vmem = pl.BlockSpec(memory_space=pltpu.VMEM)
        smem = pl.BlockSpec(memory_space=pltpu.SMEM)
        hbm = pl.BlockSpec(memory_space=pl.ANY)
        dma = pltpu.SemaphoreType.DMA
        mag, hist, stat = pl.pallas_call(
            lambda *refs: kernel(nx, ny, nz, cells, *refs),
            name="field",
            out_shape=(
                jax.ShapeDtypeStruct(x.shape, F32),
                jax.ShapeDtypeStruct((2, 128), F32),
                jax.ShapeDtypeStruct((1, 128), F32),
            ),
            in_specs=[smem, smem, hbm],
            out_specs=(hbm, vmem, vmem),
            scratch_shapes=[
                pltpu.VMEM((zs + 8, ys + 16, xs), F32),
                pltpu.VMEM((zs // 2, 8, xs), F32),
                pltpu.VMEM((zs // 2, 8, xs), F32),
                pltpu.VMEM((zs // 2, 8, xs), F32),
                pltpu.VMEM((zs // 2, 8, xs), F32),
                pltpu.VMEM((zs, ys, xs), F32),
                pltpu.VMEM((8 * COARSE, 16 * COLS), F32),
                pltpu.VMEM((4, 128), F32),
                pltpu.VMEM((nx * nz, 4, 128), F32),
                pltpu.VMEM((ny, 4, 128), F32),
                dma, dma, dma((6,)), dma((6,)),
                dma((nx * nz - 1,)), dma((nx * nz - 1,)), dma((ny - 1,)), dma((ny - 1,)),
            ],
            compiler_params=pltpu.CompilerParams(collective_id=0, has_side_effects=True),
        )(first, beyond, x)
        return mag, hist.reshape(BINS), stat[0, :4]

    return jax.shard_map(
        on_device, mesh=mesh,
        in_specs=(P("gz", "gy", "gx"), P(), P()),
        out_specs=(P("gz", "gy", "gx"), P(), P()),
        check_vma=False,
    )
```

time: 226 us -> 53.6 us (0.24)
  the two profiles are of different devices: /device:TPU:24 before, /device:TPU:1 now
where the time goes in v1:
time: 53.6 us; the launch traced here: 53.4 us
  Pallas kernels  47.5 us (89%)
  local copies, waits for them, and re-layouts  3.95 us (7%)
  between operations  1.94 us (4%)
    pallas_call x1, Pallas kernels, on_device(): pl.pallas_call(lambda *refs: kernel(nx, ny, nz, cells, *refs), name='fiel...  47.5 us
    unnamed x6, local copies, waits for them, and re-layouts  3.44 us

profile of v1, /device:TPU:1, one launch (start us, length us, event | category | flops | bytes accessed | tf_op | source)
XLA Modules:
  0.0 53.4 jit_solution(17320659412294149603)
XLA Ops:
  1.9 47.5 %field.1 = (f32[32,64,128]{2,1,0:T(8,128)}, f32[2,128]{1,0:T(2,128)}, f32[1,128]{1,0:T(1,128)}) custom-call(s32[1]{0:T(128)S(6)} %copy.8.refs_0_, s32[1]{0:T(128)S(6)} %copy.9.refs_1_, f32[32,64,128]{2,1,0:T(8,128)} %refs_2_.1), custom_call_target="tpu_custom_call" | custom-call | tf_op jit(solution)/shard_map/field/pallas_call | solution.py:229
  49.5 0.0 copy-start.1
  49.5 0.6 %copy-done.1 = f32[1,128]{1,0:T(1,128)S(1)} copy-done((f32[1,128]{1,0:T(1,128)S(1)}, f32[1,128]{1,0:T(1,128)}, u32[]{:S(2)}) %copy-start.1) | copy-done | bytes 536
  50.1 0.5 slice_bitcast_fusion
  50.6 0.0 copy-start
  50.6 2.3 %copy.10 = f32[32,64,128]{2,1,0:T(8,128)} copy(f32[32,64,128]{2,1,0:T(8,128)} %get-tuple-element.12) | data formatting | bytes 2097152
  52.9 0.0 copy-done
  52.9 0.6 %copy.11 = f32[256]{0:T(256)} copy(f32[256]{0:T(256)S(1)} %bitcast.3) | data formatting | bytes 2048
Async XLA Ops:
  49.5 0.6 %copy-start.1 = (f32[1,128]{1,0:T(1,128)S(1)}, f32[1,128]{1,0:T(1,128)}, u32[]{:S(2)}) copy-start(f32[1,128]{1,0:T(1,128)} %get-tuple-element.8) | copy-start | bytes 1540
  50.6 2.3 %copy-start = (f32[2,128]{1,0:T(2,128)S(1)}, f32[2,128]{1,0:T(2,128)}, u32[]{:S(2)}) copy-start(f32[2,128]{1,0:T(2,128)} %get-tuple-element.7) | copy-start | bytes 3076

commit v2 on v1

v2 whole, which is shorter than its diff:
```python
import jax
import jax.numpy as jnp
from jax import lax
from jax.experimental import pallas as pl
from jax.experimental.pallas import tpu as pltpu
from jax.sharding import PartitionSpec as P

BINS = 256
RANGE = 12.0
COEF = (0.8, -0.2, 4.0 / 105.0, -1.0 / 280.0)
RATIO = tuple(c / COEF[0] for c in COEF)
FINE = 10
COARSE = 26
ROWS, COLS = 8 * COARSE, 24 * FINE
ROUND = 49152.0
MESH = pl.DeviceIdType.MESH
BF = jnp.bfloat16
F32 = jnp.float32


def iota(shape, dim):
    return lax.broadcasted_iota(jnp.int32, shape, dim)


def twice(v):
    return jnp.concatenate([v, v], axis=0).astype(BF)


def kernel(nx, ny, nz, cells, window, x_ref, mag, fin,
           xe, xph, xpl, xrh, xrl, yph, ypl, yrh, yrl, corh, corl, pick, acc, own, plane, line,
           in_sem, halo_send, halo_recv, plane_sem, line_sem, known):
    gx, gy, gz = lax.axis_index("gx"), lax.axis_index("gy"), lax.axis_index("gz")
    zs, ys, lanes = x_ref.shape
    tiles = ys // 8

    def away(axis, d):
        here, size = {"gx": (gx, nx), "gy": (gy, ny), "gz": (gz, nz)}[axis]
        return {axis: lax.rem(here + d % size, size)}

    def tell(sem, peers):
        for peer in peers:
            pl.semaphore_signal(sem, inc=1, device_id=peer, device_id_type=MESH)

    near = [away(axis, d) for axis in ("gx", "gy", "gz") for d in (1, -1)]
    barrier = pltpu.get_barrier_semaphore()
    load = pltpu.make_async_copy(x_ref, xe.at[pl.ds(4, zs), pl.ds(8, ys), :], in_sem)
    load.start()
    tell(barrier, near)

    lane = iota((8, lanes), 1)
    sub = iota((8, lanes), 0)
    group, part = lane // 4, lane % 4
    acc[...] = jnp.zeros_like(acc)
    kind, digit = iota((COLS, BINS), 0) // (8 * FINE), (iota((COLS, BINS), 0) // 8) % FINE
    bin_ = iota((COLS, BINS), 1)
    picked = jnp.where(digit == bin_ % FINE, jnp.where(kind == 0, 1.0, -1.0), 0.0)
    moved = jnp.where((digit == (bin_ + FINE - 1) % FINE) & (kind > 0), 1.0, 0.0)
    pick[:, :BINS] = picked.astype(BF)
    pick[:, BINS:] = moved.astype(BF)

    load.wait()

    def pack_y(i, carry):
        z = 4 + 2 * i
        yph[i] = jnp.where(sub < 4, xe[z, pl.ds(ys + 4, 8), :], xe[z + 1, pl.ds(ys, 8), :])
        ypl[i] = jnp.where(sub < 4, xe[z, pl.ds(8, 8), :], xe[z + 1, pl.ds(4, 8), :])
        return carry

    def pack_x(p, carry):
        high = jnp.zeros((8, lanes), F32)
        low = jnp.zeros((8, lanes), F32)
        for g in range(32):
            tile = xe[4 + 4 * p + g // 8, pl.ds(8 + 8 * (g % 8), 8), :]
            high = jnp.where(group == g, pltpu.roll(tile, (4 + 4 * g) % lanes, 1), high)
            low = jnp.where(group == g, pltpu.roll(tile, 4 * g, 1) if g else tile, low)
        xph[p] = high
        xpl[p] = low
        return carry

    lax.fori_loop(0, zs // 2, pack_y, 0)
    lax.fori_loop(0, zs // 4, pack_x, 0)
    pl.semaphore_wait(barrier, len(near))

    def send(i, src, dst, peer):
        copy = pltpu.make_async_remote_copy(
            src_ref=src, dst_ref=dst, send_sem=halo_send.at[i], recv_sem=halo_recv.at[i],
            device_id=peer, device_id_type=MESH)
        copy.start()
        return copy

    mid_y = pl.ds(8, ys)
    sides = [
        send(0, xph, xrh, away("gx", 1)),
        send(1, xpl, xrl, away("gx", -1)),
        send(2, yph, yrh, away("gy", 1)),
        send(3, ypl, yrl, away("gy", -1)),
    ]
    depths = [
        send(4, xe.at[pl.ds(zs, 4), mid_y, :], xe.at[pl.ds(0, 4), mid_y, :], away("gz", 1)),
        send(5, xe.at[pl.ds(4, 4), mid_y, :], xe.at[pl.ds(zs + 4, 4), mid_y, :], away("gz", -1)),
    ]
    tell(known.at[0], near)
    for copy in sides:
        copy.wait()

    def unpack_y(i, carry):
        z = 4 + 2 * i
        below, above = yrh[i], yrl[i]
        xe[z, pl.ds(4, 4), :] = below[:4]
        xe[z + 1, pl.ds(4, 4), :] = below[4:]
        xe[z, pl.ds(ys + 8, 4), :] = above[:4]
        xe[z + 1, pl.ds(ys + 8, 4), :] = above[4:]
        return carry

    def correct(p, carry):
        left = xrh[p] - xph[p]
        right = xrl[p] - xpl[p]
        ahead = RATIO[3] * right
        behind = RATIO[3] * left
        for k in range(1, 4):
            ahead = ahead + jnp.where(part >= 4 - k, RATIO[k - 1] * pltpu.roll(right, 4 - k, 1), 0.0)
            behind = behind + jnp.where(part < k, RATIO[k - 1] * pltpu.roll(left, lanes - 4 + k, 1), 0.0)
        corh[p] = ahead
        corl[p] = -behind
        return carry

    lax.fori_loop(0, zs // 2, unpack_y, 0)
    lax.fori_loop(0, zs // 4, correct, 0)
    pl.semaphore_wait(known.at[0], len(near))
    tell(known.at[1], [away(axis, d) for axis in ("gy", "gz") for d in (2, -2)])

    first, upper = window[:1], window[1:]
    lower = first - 1.0
    half = jnp.where(iota((16, lanes), 0) < 8, 0.0, 1.0).astype(BF)
    one = jnp.ones((16, lanes), BF)
    zero = jnp.zeros((16, lanes), BF)

    def planes(turn, carry):
        total, most, least = carry
        p = lax.rem(turn + 1, zs // 4)
        product = None
        for sub_z in range(4):
            z = 4 * p + sub_z
            left, right = [], []
            for t in range(tiles):
                row = 8 + 8 * t
                g = 8 * sub_z + t
                tile = xe[4 + z, pl.ds(row, 8), :]
                rx = jnp.where(lane >= lanes - 4, pltpu.roll(corh[p], (lanes - 4 - 4 * g) % lanes, 1),
                               jnp.where(lane < 4, pltpu.roll(corl[p], (lanes - 4 * g) % lanes, 1), 0.0))
                ry, rz = None, None
                for k, c in enumerate(RATIO, start=1):
                    dz = xe[4 + z + k, pl.ds(row, 8), :] - xe[4 + z - k, pl.ds(row, 8), :]
                    dy = xe[4 + z, pl.ds(row + k, 8), :] - xe[4 + z, pl.ds(row - k, 8), :]
                    dx = pltpu.roll(tile, lanes - k, 1) - pltpu.roll(tile, k, 1)
                    rz = dz if rz is None else rz + c * dz
                    ry = dy if ry is None else ry + c * dy
                    rx = rx + (dx if k == 1 else c * dx)
                square = (rz * rz + ry * ry + rx * rx) * (COEF[0] * COEF[0]) + 1.0
                m = square * lax.rsqrt(square) - 1.0
                mag[z, pl.ds(8 * t, 8), :] = m
                q = jnp.minimum(jnp.maximum(m * (BINS / RANGE) - 0.5, 0.0), BINS - 1.0)
                low = jnp.minimum(jnp.floor(q), BINS - 2.0)
                frac = q - low
                weight = jnp.maximum(jnp.minimum(jnp.minimum(q - lower, 1.0), upper - q), 0.0)
                wm = weight * m
                total = total + wm
                most = jnp.maximum(most, wm)
                least = jnp.minimum(least, m + RANGE * (1.0 - weight))
                coarse = jnp.floor((low + 0.5) * (1.0 / FINE))
                fine = low - FINE * coarse
                big = (frac + ROUND) - ROUND
                c2 = twice(coarse) - half
                f2 = twice(fine) - half
                th, tl = twice(big), twice(frac - big)
                left.append(jnp.concatenate(
                    [jnp.where(c2 == 2.0 * i, one, zero) for i in range(COARSE // 2)], axis=0))
                here = [f2 == 2.0 * i for i in range(FINE // 2)]
                right.append(jnp.concatenate(
                    [jnp.where(h, v, zero) for v in (one, th, tl) for h in here], axis=0))
            dot = lax.dot_general(
                jnp.concatenate(left, axis=1), jnp.concatenate(right, axis=1),
                (((1,), (1,)), ((), ())), preferred_element_type=F32)
            product = dot if product is None else product + dot
        acc[...] += product
        return total, most, least

    start = jnp.zeros((8, lanes), F32)
    state = (start, start - jnp.inf, start + jnp.inf)
    inner = zs // 4 - 2
    state = lax.fori_loop(0, inner, planes, state)
    for copy in depths:
        copy.wait()
    pl.semaphore_wait(known.at[1], 4)
    tell(known.at[2], [away("gy", 4), away("gy", -4)] + [away("gx", d) for d in range(1, nx)])
    total, most, least = lax.fori_loop(inner, zs // 4, planes, state)

    prod = jnp.where(iota((ROWS, COLS), 0) % 8 == iota((ROWS, COLS), 1) % 8, acc[...], 0.0)
    table = jnp.sum(prod.reshape(COARSE, 8, COLS), axis=1)
    one_part = table.astype(BF)
    rest = table - one_part.astype(F32)
    two_part = rest.astype(BF)
    three_part = (rest - two_part.astype(F32)).astype(BF)
    crow = iota((COARSE, BINS), 0)
    cbin = iota((COARSE, BINS), 1)

    def spread(v):
        return lax.dot_general(v, pick[...], (((1,), (0,)), ((), ())), preferred_element_type=F32)

    wide = spread(one_part) + spread(two_part) + spread(three_part)
    counts = jnp.sum(
        jnp.where(crow == cbin // FINE, wide[:, :BINS], 0.0)
        + jnp.where(crow + 1 == (cbin + FINE - 1) // FINE, wide[:, BINS:], 0.0),
        axis=0, keepdims=True)
    r4, l4 = iota((4, 128), 0), iota((4, 128), 1)
    mine = jnp.where(r4 == 0, counts[:, :128], jnp.where(r4 == 1, counts[:, 128:], 0.0))
    mine = jnp.where((r4 == 2) & (l4 == 0), jnp.sum(total), mine)
    mine = jnp.where((r4 == 2) & (l4 == 1), jnp.max(most), mine)
    mine = jnp.where((r4 == 2) & (l4 == 2), -jnp.min(least), mine)
    is_max = (r4 == 2) & (l4 >= 1)

    def exchange(value, buffer, place, peers, sems):
        own[...] = value
        buffer[place] = value
        for peer in peers:
            pltpu.make_async_remote_copy(
                src_ref=own, dst_ref=buffer.at[place], send_sem=sems.at[0], recv_sem=sems.at[1],
                device_id=peer, device_id_type=MESH).start()
        every = buffer.at[pl.ds(0, len(peers))]
        pltpu.make_async_copy(every, every, sems.at[1]).wait()
        pltpu.make_async_copy(every, every, sems.at[0]).wait()
        added, top = buffer[0], buffer[0]
        for i in range(1, buffer.shape[0]):
            added = added + buffer[i]
            top = jnp.maximum(top, buffer[i])
        return jnp.where(is_max, top, added)

    pl.semaphore_wait(known.at[2], nx + 1)
    mine = exchange(mine, plane, gx * nz + gz,
                    [away("gx", dx) | away("gz", dz) for dx in range(nx) for dz in range(nz) if dx or dz],
                    plane_sem)
    mine = exchange(mine, line, gy, [away("gy", d) for d in range(1, ny)], line_sem)

    bins = (l4 + 128 * r4).astype(F32)
    count = jnp.sum(jnp.where((r4 < 2) & (bins >= first) & (bins < upper), mine, 0.0))

    def lane_of(i):
        return jnp.sum(jnp.where((r4 == 2) & (l4 == i), mine, 0.0))

    stats = jnp.where(l4 == 0, -lane_of(2), jnp.where(
        l4 == 1, lane_of(1), jnp.where(l4 == 2, lane_of(0) / cells, count / cells)))
    fin[...] = jnp.where(r4 < 2, mine * (BINS / cells), stats)


def finish(mag, fin, mag_ref, hist_ref, stat_ref, sem):
    store = pltpu.make_async_copy(mag, mag_ref, sem)
    store.start()
    hist_ref[...] = fin[:2]
    stat_ref[...] = fin[2:3, :4]
    store.wait()


def solution(mesh):
    nx, ny, nz = mesh.shape["gx"], mesh.shape["gy"], mesh.shape["gz"]

    def on_device(x, first, beyond):
        zs, ys, xs = x.shape
        cells = float(zs * ys * xs * nx * ny * nz)
        vmem = pl.BlockSpec(memory_space=pltpu.VMEM)
        hbm = pl.BlockSpec(memory_space=pltpu.HBM)
        dma = pltpu.SemaphoreType.DMA
        x_pack = pltpu.VMEM((zs // 4, 8, xs), F32)
        y_pack = pltpu.VMEM((zs // 2, 8, xs), F32)
        window = jnp.concatenate([jnp.broadcast_to(v.astype(F32), (1, xs)) for v in (first, beyond)])
        window = pltpu.with_memory_space_constraint(window, pltpu.VMEM)
        mag, fin = pl.pallas_call(
            lambda *refs: kernel(nx, ny, nz, cells, *refs),
            name="field",
            out_shape=(pltpu.VMEM(x.shape, F32), pltpu.VMEM((4, 128), F32)),
            in_specs=[vmem, hbm],
            out_specs=(vmem, vmem),
            scratch_shapes=[
                pltpu.VMEM((zs + 8, ys + 16, xs), F32),
                x_pack, x_pack, x_pack, x_pack,
                y_pack, y_pack, y_pack, y_pack,
                x_pack, x_pack,
                pltpu.VMEM((COLS, 2 * BINS), BF),
                pltpu.VMEM((ROWS, COLS), F32),
                pltpu.VMEM((4, 128), F32),
                pltpu.VMEM((nx * nz, 4, 128), F32),
                pltpu.VMEM((ny, 4, 128), F32),
                dma, dma((6,)), dma((6,)), dma((2,)), dma((2,)),
                pltpu.SemaphoreType.REGULAR((3,)),
            ],
            compiler_params=pltpu.CompilerParams(collective_id=0, has_side_effects=True),
        )(window, x)
        mag, fin = (pltpu.with_memory_space_constraint(v, pltpu.VMEM) for v in (mag, fin))
        mag, hist, stat = pl.pallas_call(
            finish,
            name="finish",
            out_shape=(
                jax.ShapeDtypeStruct(x.shape, F32),
                jax.ShapeDtypeStruct((2, 128), F32),
                jax.ShapeDtypeStruct((1, 4), F32),
            ),
            in_specs=[vmem, vmem],
            out_specs=(hbm, vmem, vmem),
            scratch_shapes=[dma],
        )(mag, fin)
        return mag, hist.reshape(BINS), stat.reshape(4)

    return jax.shard_map(
        on_device, mesh=mesh,
        in_specs=(P("gz", "gy", "gx"), P(), P()),
        out_specs=(P("gz", "gy", "gx"), P(), P()),
        check_vma=False,
    )
```

time: 53.6 us -> 44.6 us (0.83)
  Pallas kernels: 47.5 us -> 42.4 us
  local copies, waits for them, and re-layouts: 3.95 us -> 0.07 us
    pallas_call x1, Pallas kernels: 47.5 us -> 40.8 us  [on_device(): pl.pallas_call(lambda *refs: kernel(nx, ny, nz, cells, *refs), name='fiel...]
    unnamed x6 -> x0, local copies, waits for them, and re-layouts: 3.44 us -> none
    pallas_call x0 -> x1, Pallas kernels: none -> 1.54 us  [on_device(): pl.pallas_call(finish, name='finish', out_shape=(jax.ShapeDtypeStruct(x.s...]
where the time goes in v2:
time: 44.6 us; the launch traced here: 44.4 us
  Pallas kernels  42.4 us (95%)
  between operations  1.94 us (4%)
    pallas_call x1, Pallas kernels, on_device(): pl.pallas_call(lambda *refs: kernel(nx, ny, nz, cells, *refs), name='fiel...  40.8 us
    pallas_call x1, Pallas kernels, on_device(): pl.pallas_call(finish, name='finish', out_shape=(jax.ShapeDtypeStruct(x.s...  1.54 us

profile of v2, /device:TPU:1, one launch (start us, length us, event | category | flops | bytes accessed | tf_op | source)
XLA Modules:
  0.0 44.4 jit_solution(12222329226437381497)
XLA Ops:
  1.9 0.1 concatenate.6.refs_0_
  2.0 40.8 %field.1 = (f32[32,64,128]{2,1,0:T(8,128)S(1)}, f32[4,128]{1,0:T(4,128)S(1)}) custom-call(f32[2,128]{1,0:T(2,128)S(1)} %concatenate.6.refs_0_, f32[32,64,128]{2,1,0:T(8,128)} %refs_1_.1), custom_call_target="tpu_custom_call" | custom-call | tf_op jit(solution)/shard_map/field/pallas_call | solution.py:276
  42.8 1.5 %finish.1 = (f32[32,64,128]{2,1,0:T(8,128)}, f32[2,128]{1,0:T(2,128)}, f32[1,4]{1,0:T(1,128)}) custom-call(f32[32,64,128]{2,1,0:T(8,128)S(1)} %get-tuple-element.8.mag, f32[4,128]{1,0:T(4,128)S(1)} %get-tuple-element.9.fin), custom_call_target="tpu_custom_call" | custom-call | tf_op jit(solution)/shard_map/finish/pallas_call | solution.py:298
  (1 shorter events, 0.0 us)

commit v3 on v2

v3 whole, which is shorter than its diff:
```python
import jax
import jax.numpy as jnp
from jax import lax
from jax.experimental import pallas as pl
from jax.experimental.pallas import tpu as pltpu
from jax.sharding import PartitionSpec as P

BINS = 256
RANGE = 12.0
COEF = (0.8, -0.2, 4.0 / 105.0, -1.0 / 280.0)
RATIO = tuple(c / COEF[0] for c in COEF)
FINE = 10
COARSE = 26
ROWS, COLS = 8 * COARSE, 24 * FINE
ROUND = 49152.0
MESH = pl.DeviceIdType.MESH
BF = jnp.bfloat16
F32 = jnp.float32


def iota(shape, dim):
    return lax.broadcasted_iota(jnp.int32, shape, dim)


def twice(v):
    return jnp.concatenate([v, v], axis=0).astype(BF)


def kernel(nx, ny, nz, cells, window, x_ref, mag, hist, stat,
           xe, xp, xl, xr, yph, ypl, yrh, yrl, flat, bend, rim, pick, acc, own, plane, line,
           in_sem, halo_send, halo_recv, plane_sem, line_sem, known):
    gx, gy, gz = lax.axis_index("gx"), lax.axis_index("gy"), lax.axis_index("gz")
    zs, ys, lanes = x_ref.shape
    tiles = ys // 8

    def away(axis, d):
        here, size = {"gx": (gx, nx), "gy": (gy, ny), "gz": (gz, nz)}[axis]
        return {axis: lax.rem(here + d % size, size)}

    def tell(sem, peers):
        for peer in peers:
            pl.semaphore_signal(sem, inc=1, device_id=peer, device_id_type=MESH)

    near = [away(axis, d) for axis in ("gx", "gy", "gz") for d in (1, -1)]
    barrier = pltpu.get_barrier_semaphore()
    load = pltpu.make_async_copy(x_ref, xe.at[pl.ds(4, zs), pl.ds(8, ys), :], in_sem)
    load.start()
    tell(barrier, near)

    lane = iota((8, lanes), 1)
    sub = iota((8, lanes), 0)
    group, part = lane // 8, lane % 8
    acc[...] = jnp.zeros_like(acc)
    kind, digit = iota((COLS, BINS), 0) // (8 * FINE), (iota((COLS, BINS), 0) // 8) % FINE
    bin_ = iota((COLS, BINS), 1)
    picked = jnp.where(digit == bin_ % FINE, jnp.where(kind == 0, 1.0, -1.0), 0.0)
    moved = jnp.where((digit == (bin_ + FINE - 1) % FINE) & (kind > 0), 1.0, 0.0)
    pick[:, :BINS] = picked.astype(BF)
    pick[:, BINS:] = moved.astype(BF)

    load.wait()

    def pack_y(i, carry):
        z = 4 + 2 * i
        yph[i] = jnp.where(sub < 4, xe[z, pl.ds(ys + 4, 8), :], xe[z + 1, pl.ds(ys, 8), :])
        ypl[i] = jnp.where(sub < 4, xe[z, pl.ds(8, 8), :], xe[z + 1, pl.ds(4, 8), :])
        return carry

    def pack_x(p, carry):
        packed = jnp.zeros((8, lanes), F32)
        for g in range(16):
            tile = xe[4 + 2 * p + g // 8, pl.ds(8 + 8 * (g % 8), 8), :]
            packed = jnp.where(group == g, pltpu.roll(tile, (4 + 8 * g) % lanes, 1), packed)
        xp[p] = packed
        return carry

    lax.fori_loop(0, zs // 2, pack_y, 0)
    lax.fori_loop(0, zs // 2, pack_x, 0)
    pl.semaphore_wait(barrier, len(near))

    def send(i, src, dst, peer):
        copy = pltpu.make_async_remote_copy(
            src_ref=src, dst_ref=dst, send_sem=halo_send.at[i], recv_sem=halo_recv.at[i],
            device_id=peer, device_id_type=MESH)
        copy.start()
        return copy

    mid_y = pl.ds(8, ys)
    rows_y = [
        send(2, yph, yrh, away("gy", 1)),
        send(3, ypl, yrl, away("gy", -1)),
    ]
    depths = [
        send(4, xe.at[pl.ds(zs, 4), mid_y, :], xe.at[pl.ds(0, 4), mid_y, :], away("gz", 1)),
        send(5, xe.at[pl.ds(4, 4), mid_y, :], xe.at[pl.ds(zs + 4, 4), mid_y, :], away("gz", -1)),
    ]
    rows_x = [
        send(0, xp, xl, away("gx", 1)),
        send(1, xp, xr, away("gx", -1)),
    ]
    tell(known.at[0], near)

    def unpack_y(i, carry):
        z = 4 + 2 * i
        below, above = yrh[i], yrl[i]
        xe[z, pl.ds(4, 4), :] = below[:4]
        xe[z + 1, pl.ds(4, 4), :] = below[4:]
        xe[z, pl.ds(ys + 8, 4), :] = above[:4]
        xe[z + 1, pl.ds(ys + 8, 4), :] = above[4:]
        return carry

    first, upper = window[:1], window[1:]
    lower = first - 1.0
    half = jnp.where(iota((16, lanes), 0) < 8, 0.0, 1.0).astype(BF)
    one = jnp.ones((16, lanes), BF)
    zero = jnp.zeros((16, lanes), BF)

    edge = (lane < 4) | (lane >= lanes - 4)

    def slope(z, t):
        row = 8 + 8 * t
        tile = xe[4 + z, pl.ds(row, 8), :]
        rx, ry, rz = None, None, None
        for k, c in enumerate(RATIO, start=1):
            dz = xe[4 + z + k, pl.ds(row, 8), :] - xe[4 + z - k, pl.ds(row, 8), :]
            dy = xe[4 + z, pl.ds(row + k, 8), :] - xe[4 + z, pl.ds(row - k, 8), :]
            dx = pltpu.roll(tile, lanes - k, 1) - pltpu.roll(tile, k, 1)
            rz = dz if rz is None else rz + c * dz
            ry = dy if ry is None else ry + c * dy
            rx = dx if rx is None else rx + c * dx
        return rz * rz + ry * ry, rx

    def cell(square, state, masked):
        total, most, least = state
        square = square * (COEF[0] * COEF[0]) + 1.0
        m = square * lax.rsqrt(square) - 1.0
        q = jnp.minimum(jnp.maximum(m * (BINS / RANGE) - 0.5, 0.0), BINS - 1.0)
        low = jnp.floor(q)
        frac = q - low
        weight = jnp.maximum(jnp.minimum(jnp.minimum(q - lower, 1.0), upper - q), 0.0)
        if masked:
            weight = jnp.where(edge, 0.0, weight)
        wm = weight * m
        under = m - RANGE * weight
        if masked:
            under = jnp.where(edge, jnp.inf, under)
        state = total + wm, jnp.maximum(most, wm), jnp.minimum(least, under)
        coarse = jnp.floor((low + 0.5) * (1.0 / FINE))
        fine = low - FINE * coarse
        if masked:
            coarse = jnp.where(edge, -64.0, coarse)
        th = twice(frac)
        tl = twice(frac - th[:8].astype(F32))
        c2 = twice(coarse) - half
        f2 = twice(fine) - half
        here = [f2 == 2.0 * i for i in range(FINE // 2)]
        left = jnp.concatenate([jnp.where(c2 == 2.0 * i, one, zero) for i in range(COARSE // 2)], axis=0)
        right = jnp.concatenate([jnp.where(h, v, zero) for v in (one, th, tl) for h in here], axis=0)
        return m, state, left, right

    def gather(pairs):
        product = None
        for at in range(0, len(pairs), 8):
            left, right = zip(*pairs[at:at + 8])
            dot = lax.dot_general(
                jnp.concatenate(left, axis=1), jnp.concatenate(right, axis=1),
                (((1,), (1,)), ((), ())), preferred_element_type=F32)
            product = dot if product is None else product + dot
        acc[...] += product

    def body(places, state, chosen, fresh):
        pairs = []
        for z, odd in places:
            if not odd:
                flats = jnp.zeros((8, lanes), F32) if fresh else flat[z // 2]
                bends = jnp.zeros((8, lanes), F32) if fresh else bend[z // 2]
            for t in chosen:
                g = 8 * odd + t
                square, rx = slope(z, t)
                flats = jnp.where(group == g, pltpu.roll(square, (4 + 8 * g) % lanes, 1), flats)
                bends = jnp.where(group == g, pltpu.roll(rx, (4 + 8 * g) % lanes, 1), bends)
                m, state, left, right = cell(square + rx * rx, state, True)
                mag[z, pl.ds(8 * t, 8), :] = m
                pairs.append((left, right))
            if odd:
                flat[z // 2] = flats
                bend[z // 2] = bends
        return pairs, state

    inner = range(1, tiles - 1)
    outer = (0, tiles - 1)

    def middle(turn, state):
        @pl.when(turn == 1)
        def _():
            pl.semaphore_wait(known.at[0], len(near))
            tell(known.at[1], [away(axis, d) for axis in ("gy", "gz") for d in (2, -2)])

        pairs, state = body([(4 + 8 * turn + i, i % 2) for i in range(8)], state, inner, True)
        gather(pairs)
        return state

    start = jnp.zeros((8, lanes), F32)
    state = (start, start - jnp.inf, start + jnp.inf)
    thirds = (zs - 8) // 8
    state = lax.fori_loop(0, thirds, middle, state)
    pl.semaphore_wait(known.at[1], 4)
    tell(known.at[2], [away("gy", 4), away("gy", -4)] + [away("gx", d) for d in range(1, nx)])
    for copy in rows_y + depths + rows_x:
        copy.wait()
    lax.fori_loop(0, zs // 2, unpack_y, 0)

    pairs, state = body([(z, z % 2) for z in range(4, zs - 4)], state, outer, False)
    more, state = body([(z, z % 2) for z in range(zs) if z < 4 or z >= zs - 4], state, range(tiles), True)
    pairs = pairs + more
    for p in range(zs // 2):
        e = jnp.where(part < 4, xl[p], xr[p]) - xp[p]
        high = jnp.where(part >= 4, e, 0.0)
        low = jnp.where(part < 4, e, 0.0)
        ahead, behind = 0.0, 0.0
        for k, c in enumerate(RATIO, start=1):
            ahead = ahead + c * pltpu.roll(high, lanes - k, 1)
            behind = behind + c * pltpu.roll(low, k, 1)
        rx = bend[p] + jnp.where(part < 4, ahead, -behind)
        m, state, left, right = cell(flat[p] + rx * rx, state, False)
        rim[p] = m
        pairs.append((left, right))
    gather(pairs)
    total, most, least = state

    def mend(p, carry):
        for g in range(16):
            place = (2 * p + g // 8, pl.ds(8 * (g % 8), 8))
            mag[place] = jnp.where(edge, pltpu.roll(rim[p], (lanes - 4 - 8 * g) % lanes, 1), mag[place])
        return carry

    prod = jnp.where(iota((ROWS, COLS), 0) % 8 == iota((ROWS, COLS), 1) % 8, acc[...], 0.0)
    table = jnp.sum(prod.reshape(COARSE, 8, COLS), axis=1)
    one_part = table.astype(BF)
    rest = table - one_part.astype(F32)
    two_part = rest.astype(BF)
    three_part = (rest - two_part.astype(F32)).astype(BF)
    crow = iota((COARSE, BINS), 0)
    cbin = iota((COARSE, BINS), 1)

    def spread(v):
        return lax.dot_general(v, pick[...], (((1,), (0,)), ((), ())), preferred_element_type=F32)

    wide = spread(one_part) + spread(two_part) + spread(three_part)
    counts = jnp.sum(
        jnp.where(crow == cbin // FINE, wide[:, :BINS], 0.0)
        + jnp.where(crow + 1 == (cbin + FINE - 1) // FINE, wide[:, BINS:], 0.0),
        axis=0, keepdims=True)
    r4, l4 = iota((3, 128), 0), iota((3, 128), 1)
    mine = jnp.where(r4 == 0, counts[:, :128], jnp.where(r4 == 1, counts[:, 128:], 0.0))
    mine = jnp.where((r4 == 2) & (l4 == 0), jnp.sum(total), mine)
    mine = jnp.where((r4 == 2) & (l4 == 1), jnp.max(most), mine)
    mine = jnp.where((r4 == 2) & (l4 == 2), -RANGE - jnp.min(least), mine)
    is_max = (r4 == 2) & (l4 >= 1)

    def exchange(value, buffer, place, peers, sems, work=None):
        own[...] = value
        buffer[place] = value
        for peer in peers:
            pltpu.make_async_remote_copy(
                src_ref=own, dst_ref=buffer.at[place], send_sem=sems.at[0], recv_sem=sems.at[1],
                device_id=peer, device_id_type=MESH).start()
        if work is not None:
            work()
        every = buffer.at[pl.ds(0, len(peers))]
        pltpu.make_async_copy(every, every, sems.at[1]).wait()
        pltpu.make_async_copy(every, every, sems.at[0]).wait()
        added, top = buffer[0], buffer[0]
        for i in range(1, buffer.shape[0]):
            added = added + buffer[i]
            top = jnp.maximum(top, buffer[i])
        return jnp.where(is_max, top, added)

    pl.semaphore_wait(known.at[2], nx + 1)
    mine = exchange(mine, plane, gx * nz + gz,
                    [away("gx", dx) | away("gz", dz) for dx in (2, 1, 3, 0) for dz in (2, 6, 5, 3, 4, 1, 7, 0) if dx or dz],
                    plane_sem, lambda: lax.fori_loop(0, zs // 2, mend, 0))
    mine = exchange(mine, line, gy, [away("gy", d) for d in (8, 7, 9, 6, 10, 5, 11, 4, 12, 3, 13, 2, 14, 1, 15)], line_sem)

    bins = (l4 + 128 * r4).astype(F32)
    count = jnp.sum(jnp.where((r4 < 2) & (bins >= first) & (bins < upper), mine, 0.0))

    def lane_of(i):
        return jnp.sum(jnp.where((r4 == 2) & (l4 == i), mine, 0.0))

    l1 = iota((1, 4), 1)
    hist[...] = mine[:2] * (BINS / cells)
    stat[...] = jnp.where(l1 == 0, -lane_of(2), jnp.where(
        l1 == 1, lane_of(1), jnp.where(l1 == 2, lane_of(0) / cells, count / cells)))


def finish(mag, hist, stat, mag_ref, hist_ref, stat_ref, sems):
    copies = [
        pltpu.make_async_copy(source, target, sems.at[i])
        for i, (source, target) in enumerate(((mag, mag_ref), (hist, hist_ref), (stat, stat_ref)))
    ]
    for copy in copies:
        copy.start()
    for copy in copies:
        copy.wait()


def solution(mesh):
    nx, ny, nz = mesh.shape["gx"], mesh.shape["gy"], mesh.shape["gz"]

    def on_device(x, first, beyond):
        zs, ys, xs = x.shape
        cells = float(zs * ys * xs * nx * ny * nz)
        vmem = pl.BlockSpec(memory_space=pltpu.VMEM)
        hbm = pl.BlockSpec(memory_space=pltpu.HBM)
        dma = pltpu.SemaphoreType.DMA
        window = jnp.concatenate([jnp.broadcast_to(v.astype(F32), (1, xs)) for v in (first, beyond)])
        window = pltpu.with_memory_space_constraint(window, pltpu.VMEM)
        packed = pltpu.VMEM((zs // 2, 8, xs), F32)
        parts = pl.pallas_call(
            lambda *refs: kernel(nx, ny, nz, cells, *refs),
            name="field",
            out_shape=(pltpu.VMEM(x.shape, F32), pltpu.VMEM((2, 128), F32), pltpu.VMEM((1, 4), F32)),
            in_specs=[vmem, hbm],
            out_specs=(vmem, vmem, vmem),
            scratch_shapes=[
                pltpu.VMEM((zs + 8, ys + 16, xs), F32),
                packed, packed, packed,
                packed, packed, packed, packed,
                packed, packed, packed,
                pltpu.VMEM((COLS, 2 * BINS), BF),
                pltpu.VMEM((ROWS, COLS), F32),
                pltpu.VMEM((3, 128), F32),
                pltpu.VMEM((nx * nz, 3, 128), F32),
                pltpu.VMEM((ny, 3, 128), F32),
                dma, dma((6,)), dma((6,)), dma((2,)), dma((2,)),
                pltpu.SemaphoreType.REGULAR((3,)),
            ],
            compiler_params=pltpu.CompilerParams(collective_id=0, has_side_effects=True),
        )(window, x)
        parts = [pltpu.with_memory_space_constraint(v, pltpu.VMEM) for v in parts]
        mag, hist, stat = pl.pallas_call(
            finish,
            name="finish",
            out_shape=tuple(jax.ShapeDtypeStruct(v.shape, F32) for v in parts),
            in_specs=[vmem, vmem, vmem],
            out_specs=(hbm, hbm, hbm),
            scratch_shapes=[dma((3,))],
        )(*parts)
        return mag, hist.reshape(BINS), stat.reshape(4)

    return jax.shard_map(
        on_device, mesh=mesh,
        in_specs=(P("gz", "gy", "gx"), P(), P()),
        out_specs=(P("gz", "gy", "gx"), P(), P()),
        check_vma=False,
    )
```

time: 44.6 us -> 39.1 us (0.88)
  Pallas kernels: 42.4 us -> 36.9 us
    pallas_call x1, Pallas kernels: 40.8 us -> 35.9 us  [on_device(): pl.pallas_call(lambda *refs: kernel(nx, ny, nz, cells, *refs), name='fiel...]
    pallas_call x1, Pallas kernels: 1.54 us -> 1 us  [on_device(): pl.pallas_call(finish, name='finish', out_shape=tuple((jax.ShapeDtypeStru...]
where the time goes in v3:
time: 39.1 us; the launch traced here: 39 us
  Pallas kernels  36.9 us (94%)
  between operations  1.94 us (5%)
    pallas_call x1, Pallas kernels, on_device(): pl.pallas_call(lambda *refs: kernel(nx, ny, nz, cells, *refs), name='fiel...  35.9 us
    pallas_call x1, Pallas kernels, on_device(): pl.pallas_call(finish, name='finish', out_shape=tuple((jax.ShapeDtypeStru...  1 us

profile of v3, /device:TPU:1, one launch (start us, length us, event | category | flops | bytes accessed | tf_op | source)
XLA Modules:
  0.0 39.0 jit_solution(9550960646038614707)
XLA Ops:
  1.9 0.1 concatenate.6.refs_0_
  2.0 35.9 %field.1 = (f32[32,64,128]{2,1,0:T(8,128)S(1)}, f32[2,128]{1,0:T(2,128)S(1)}, f32[1,4]{1,0:T(1,128)S(1)}) custom-call(f32[2,128]{1,0:T(2,128)S(1)} %concatenate.6.refs_0_, f32[32,64,128]{2,1,0:T(8,128)} %refs_1_.1), custom_call_target="tpu_custom_call" | custom-call | tf_op jit(solution)/shard_map/field/pallas_call | solution.py:320
  38.0 1.0 %finish.1 = (f32[32,64,128]{2,1,0:T(8,128)}, f32[2,128]{1,0:T(2,128)}, f32[1,4]{1,0:T(1,128)}) custom-call(f32[32,64,128]{2,1,0:T(8,128)S(1)} %get-tuple-element.9.mag, f32[2,128]{1,0:T(2,128)S(1)} %get-tuple-element.10.hist, f32[1,4]{1,0:T(1,128)S(1)} %get-tuple-element.11.stat), custom_call_target="tpu_custom_call" | custom-call | tf_op jit(solution)/shard_map/finish/pallas_call | solution.py:342
  (1 shorter events, 0.0 us)

commit v4 on v3

--- a/solution.py
+++ b/solution.py
@@ -27,7 +27,7 @@
 
 
 def kernel(nx, ny, nz, cells, window, x_ref, mag, hist, stat,
-           xe, xp, xl, xr, yph, ypl, yrh, yrl, flat, bend, rim, pick, acc, own, plane, line,
+           xe, xp, xh, xw, xl, xr, yph, ypl, yrh, yrl, flat, bend, rim, pick, acc, own, plane, line,
            in_sem, halo_send, halo_recv, plane_sem, line_sem, known):
     gx, gy, gz = lax.axis_index("gx"), lax.axis_index("gy"), lax.axis_index("gz")
     zs, ys, lanes = x_ref.shape
@@ -44,7 +44,9 @@
     near = [away(axis, d) for axis in ("gx", "gy", "gz") for d in (1, -1)]
     barrier = pltpu.get_barrier_semaphore()
     load = pltpu.make_async_copy(x_ref, xe.at[pl.ds(4, zs), pl.ds(8, ys), :], in_sem)
-    load.start()
+    for z in range(0, zs, 4):
+        pltpu.make_async_copy(
+            x_ref.at[pl.ds(z, 4)], xe.at[pl.ds(4 + z, 4), pl.ds(8, ys), :], in_sem).start()
     tell(barrier, near)
 
     lane = iota((8, lanes), 1)
@@ -66,16 +68,17 @@
         ypl[i] = jnp.where(sub < 4, xe[z, pl.ds(8, 8), :], xe[z + 1, pl.ds(4, 8), :])
         return carry
 
-    def pack_x(p, carry):
-        packed = jnp.zeros((8, lanes), F32)
-        for g in range(16):
-            tile = xe[4 + 2 * p + g // 8, pl.ds(8 + 8 * (g % 8), 8), :]
-            packed = jnp.where(group == g, pltpu.roll(tile, (4 + 8 * g) % lanes, 1), packed)
-        xp[p] = packed
+    def pack_x(turn, carry):
+        for i in range(4):
+            p = 4 * turn + i
+            packed = jnp.zeros((8, lanes), F32)
+            for g in range(16):
+                tile = xe[4 + 2 * p + g // 8, pl.ds(8 + 8 * (g % 8), 8), :]
+                packed = jnp.where(group == g, pltpu.roll(tile, (4 + 8 * g) % lanes, 1), packed)
+            xp[p] = packed
         return carry
 
     lax.fori_loop(0, zs // 2, pack_y, 0)
-    lax.fori_loop(0, zs // 2, pack_x, 0)
     pl.semaphore_wait(barrier, len(near))
 
     def send(i, src, dst, peer):
@@ -94,11 +97,17 @@
         send(4, xe.at[pl.ds(zs, 4), mid_y, :], xe.at[pl.ds(0, 4), mid_y, :], away("gz", 1)),
         send(5, xe.at[pl.ds(4, 4), mid_y, :], xe.at[pl.ds(zs + 4, 4), mid_y, :], away("gz", -1)),
     ]
+    tell(known.at[0], near)
+    lax.fori_loop(0, zs // 8, pack_x, 0)
+    quarter = zs // 4
+    for p in range(quarter):
+        near_p, far_p = xp[p], xp[p + quarter]
+        xh[p] = jnp.where(part < 4, near_p, pltpu.roll(far_p, 4, 1))
+        xw[p] = jnp.where(part >= 4, near_p, pltpu.roll(far_p, lanes - 4, 1))
     rows_x = [
-        send(0, xp, xl, away("gx", 1)),
-        send(1, xp, xr, away("gx", -1)),
+        send(0, xh, xl, away("gx", 1)),
+        send(1, xw, xr, away("gx", -1)),
     ]
-    tell(known.at[0], near)
 
     def unpack_y(i, carry):
         z = 4 + 2 * i
@@ -109,8 +118,7 @@
         xe[z + 1, pl.ds(ys + 8, 4), :] = above[4:]
         return carry
 
-    first, upper = window[:1], window[1:]
-    lower = first - 1.0
+    lower, upper = window[:1] - 1.0, window[1:]
     half = jnp.where(iota((16, lanes), 0) < 8, 0.0, 1.0).astype(BF)
     one = jnp.ones((16, lanes), BF)
     zero = jnp.zeros((16, lanes), BF)
@@ -131,24 +139,22 @@
         return rz * rz + ry * ry, rx
 
     def cell(square, state, masked):
-        total, most, least = state
+        total, number, most, least = state
         square = square * (COEF[0] * COEF[0]) + 1.0
         m = square * lax.rsqrt(square) - 1.0
         q = jnp.minimum(jnp.maximum(m * (BINS / RANGE) - 0.5, 0.0), BINS - 1.0)
+        if masked:
+            q = jnp.where(edge, -64.0, q)
         low = jnp.floor(q)
         frac = q - low
         weight = jnp.maximum(jnp.minimum(jnp.minimum(q - lower, 1.0), upper - q), 0.0)
-        if masked:
-            weight = jnp.where(edge, 0.0, weight)
         wm = weight * m
         under = m - RANGE * weight
         if masked:
             under = jnp.where(edge, jnp.inf, under)
-        state = total + wm, jnp.maximum(most, wm), jnp.minimum(least, under)
+        state = total + wm, number + weight, jnp.maximum(most, wm), jnp.minimum(least, under)
         coarse = jnp.floor((low + 0.5) * (1.0 / FINE))
         fine = low - FINE * coarse
-        if masked:
-            coarse = jnp.where(edge, -64.0, coarse)
         th = twice(frac)
         tl = twice(frac - th[:8].astype(F32))
         c2 = twice(coarse) - half
@@ -196,14 +202,14 @@
             pl.semaphore_wait(known.at[0], len(near))
             tell(known.at[1], [away(axis, d) for axis in ("gy", "gz") for d in (2, -2)])
 
-        pairs, state = body([(4 + 8 * turn + i, i % 2) for i in range(8)], state, inner, True)
+        pairs, state = body([(4 + planes * turn + i, i % 2) for i in range(planes)], state, inner, True)
         gather(pairs)
         return state
 
     start = jnp.zeros((8, lanes), F32)
-    state = (start, start - jnp.inf, start + jnp.inf)
-    thirds = (zs - 8) // 8
-    state = lax.fori_loop(0, thirds, middle, state)
+    state = (start, start, start - jnp.inf, start + jnp.inf)
+    planes = (zs - 8) // 2
+    state = lax.fori_loop(0, 2, middle, state)
     pl.semaphore_wait(known.at[1], 4)
     tell(known.at[2], [away("gy", 4), away("gy", -4)] + [away("gx", d) for d in range(1, nx)])
     for copy in rows_y + depths + rows_x:
@@ -214,7 +220,10 @@
     more, state = body([(z, z % 2) for z in range(zs) if z < 4 or z >= zs - 4], state, range(tiles), True)
     pairs = pairs + more
     for p in range(zs // 2):
-        e = jnp.where(part < 4, xl[p], xr[p]) - xp[p]
+        west, east = xl[p % quarter], xr[p % quarter]
+        if p >= quarter:
+            west, east = pltpu.roll(west, lanes - 4, 1), pltpu.roll(east, 4, 1)
+        e = jnp.where(part < 4, west, east) - xp[p]
         high = jnp.where(part >= 4, e, 0.0)
         low = jnp.where(part < 4, e, 0.0)
         ahead, behind = 0.0, 0.0
@@ -226,7 +235,7 @@
         rim[p] = m
         pairs.append((left, right))
     gather(pairs)
-    total, most, least = state
+    total, number, most, least = state
 
     def mend(p, carry):
         for g in range(16):
@@ -253,12 +262,11 @@
         axis=0, keepdims=True)
     r4, l4 = iota((3, 128), 0), iota((3, 128), 1)
     mine = jnp.where(r4 == 0, counts[:, :128], jnp.where(r4 == 1, counts[:, 128:], 0.0))
-    mine = jnp.where((r4 == 2) & (l4 == 0), jnp.sum(total), mine)
-    mine = jnp.where((r4 == 2) & (l4 == 1), jnp.max(most), mine)
-    mine = jnp.where((r4 == 2) & (l4 == 2), -RANGE - jnp.min(least), mine)
-    is_max = (r4 == 2) & (l4 >= 1)
-
-    def exchange(value, buffer, place, peers, sems, work=None):
+    for i, v in enumerate((-RANGE - jnp.min(least), jnp.max(most), jnp.sum(total), jnp.sum(number))):
+        mine = jnp.where((r4 == 2) & (l4 == i), v, mine)
+    is_max = (r4 == 2) & (l4 < 2)
+
+    def exchange(value, own, buffer, place, peers, sems, work=None):
         own[...] = value
         buffer[place] = value
         for peer in peers:
@@ -269,7 +277,6 @@
             work()
         every = buffer.at[pl.ds(0, len(peers))]
         pltpu.make_async_copy(every, every, sems.at[1]).wait()
-        pltpu.make_async_copy(every, every, sems.at[0]).wait()
         added, top = buffer[0], buffer[0]
         for i in range(1, buffer.shape[0]):
             added = added + buffer[i]
@@ -277,21 +284,17 @@
         return jnp.where(is_max, top, added)
 
     pl.semaphore_wait(known.at[2], nx + 1)
-    mine = exchange(mine, plane, gx * nz + gz,
+    mine = exchange(mine, own.at[0], plane, gx * nz + gz,
                     [away("gx", dx) | away("gz", dz) for dx in (2, 1, 3, 0) for dz in (2, 6, 5, 3, 4, 1, 7, 0) if dx or dz],
                     plane_sem, lambda: lax.fori_loop(0, zs // 2, mend, 0))
-    mine = exchange(mine, line, gy, [away("gy", d) for d in (8, 7, 9, 6, 10, 5, 11, 4, 12, 3, 13, 2, 14, 1, 15)], line_sem)
-
-    bins = (l4 + 128 * r4).astype(F32)
-    count = jnp.sum(jnp.where((r4 < 2) & (bins >= first) & (bins < upper), mine, 0.0))
-
-    def lane_of(i):
-        return jnp.sum(jnp.where((r4 == 2) & (l4 == i), mine, 0.0))
-
-    l1 = iota((1, 4), 1)
+    mine = exchange(mine, own.at[1], line, gy, [away("gy", d) for d in (8, 7, 9, 6, 10, 5, 11, 4, 12, 3, 13, 2, 14, 1, 15)], line_sem)
+
     hist[...] = mine[:2] * (BINS / cells)
-    stat[...] = jnp.where(l1 == 0, -lane_of(2), jnp.where(
-        l1 == 1, lane_of(1), jnp.where(l1 == 2, lane_of(0) / cells, count / cells)))
+    last, l1 = mine[2:, :4], iota((1, 4), 1)
+    for buffer, sems in ((plane, plane_sem), (line, line_sem)):
+        sent = buffer.at[pl.ds(0, buffer.shape[0] - 1)]
+        pltpu.make_async_copy(sent, sent, sems.at[0]).wait()
+    stat[...] = jnp.where(l1 == 0, -last, jnp.where(l1 == 1, last, last / cells))
 
 
 def finish(mag, hist, stat, mag_ref, hist_ref, stat_ref, sems):
@@ -317,6 +320,7 @@
         window = jnp.concatenate([jnp.broadcast_to(v.astype(F32), (1, xs)) for v in (first, beyond)])
         window = pltpu.with_memory_space_constraint(window, pltpu.VMEM)
         packed = pltpu.VMEM((zs // 2, 8, xs), F32)
+        slim = pltpu.VMEM((zs // 4, 8, xs), F32)
         parts = pl.pallas_call(
             lambda *refs: kernel(nx, ny, nz, cells, *refs),
             name="field",
@@ -325,12 +329,12 @@
             out_specs=(vmem, vmem, vmem),
             scratch_shapes=[
                 pltpu.VMEM((zs + 8, ys + 16, xs), F32),
-                packed, packed, packed,
+                packed, slim, slim, slim, slim,
                 packed, packed, packed, packed,
                 packed, packed, packed,
                 pltpu.VMEM((COLS, 2 * BINS), BF),
                 pltpu.VMEM((ROWS, COLS), F32),
-                pltpu.VMEM((3, 128), F32),
+                pltpu.VMEM((2, 3, 128), F32),
                 pltpu.VMEM((nx * nz, 3, 128), F32),
                 pltpu.VMEM((ny, 3, 128), F32),
                 dma, dma((6,)), dma((6,)), dma((2,)), dma((2,)),

time: 39.1 us -> 38.1 us (0.974)
  Pallas kernels: 36.9 us -> 36 us
    pallas_call x1, Pallas kernels: 35.9 us -> 35 us  [on_device(): pl.pallas_call(lambda *refs: kernel(nx, ny, nz, cells, *refs), name='fiel...]
where the time goes in v4:
time: 38.1 us; the launch traced here: 38 us
  Pallas kernels  36 us (94%)
  between operations  1.94 us (5%)
    pallas_call x1, Pallas kernels, on_device(): pl.pallas_call(lambda *refs: kernel(nx, ny, nz, cells, *refs), name='fiel...  35 us
    pallas_call x1, Pallas kernels, on_device(): pl.pallas_call(finish, name='finish', out_shape=tuple((jax.ShapeDtypeStru...  1 us

profile of v4, /device:TPU:1, one launch (start us, length us, event | category | flops | bytes accessed | tf_op | source)
XLA Modules:
  0.0 38.0 jit_solution(7218726216935254791)
XLA Ops:
  1.9 0.1 concatenate.6.refs_0_
  2.0 35.0 %field.1 = (f32[32,64,128]{2,1,0:T(8,128)S(1)}, f32[2,128]{1,0:T(2,128)S(1)}, f32[1,4]{1,0:T(1,128)S(1)}) custom-call(f32[2,128]{1,0:T(2,128)S(1)} %concatenate.6.refs_0_, f32[32,64,128]{2,1,0:T(8,128)} %refs_1_.1), custom_call_target="tpu_custom_call" | custom-call | tf_op jit(solution)/shard_map/field/pallas_call | solution.py:324
  37.0 1.0 %finish.1 = (f32[32,64,128]{2,1,0:T(8,128)}, f32[2,128]{1,0:T(2,128)}, f32[1,4]{1,0:T(1,128)}) custom-call(f32[32,64,128]{2,1,0:T(8,128)S(1)} %get-tuple-element.9.mag, f32[2,128]{1,0:T(2,128)S(1)} %get-tuple-element.10.hist, f32[1,4]{1,0:T(1,128)S(1)} %get-tuple-element.11.stat), custom_call_target="tpu_custom_call" | custom-call | tf_op jit(solution)/shard_map/finish/pallas_call | solution.py:346
  (1 shorter events, 0.0 us)

commit v5 on v4

--- a/solution.py
+++ b/solution.py
@@ -68,17 +68,18 @@
         ypl[i] = jnp.where(sub < 4, xe[z, pl.ds(8, 8), :], xe[z + 1, pl.ds(4, 8), :])
         return carry
 
-    def pack_x(turn, carry):
-        for i in range(4):
-            p = 4 * turn + i
-            packed = jnp.zeros((8, lanes), F32)
-            for g in range(16):
-                tile = xe[4 + 2 * p + g // 8, pl.ds(8 + 8 * (g % 8), 8), :]
-                packed = jnp.where(group == g, pltpu.roll(tile, (4 + 8 * g) % lanes, 1), packed)
-            xp[p] = packed
-        return carry
-
     lax.fori_loop(0, zs // 2, pack_y, 0)
+    for p in range(zs // 2):
+        packed = jnp.zeros((8, lanes), F32)
+        for g in range(16):
+            tile = xe[4 + 2 * p + g // 8, pl.ds(8 + 8 * (g % 8), 8), :]
+            packed = jnp.where(group == g, pltpu.roll(tile, (4 + 8 * g) % lanes, 1), packed)
+        xp[p] = packed
+    quarter = zs // 4
+    for p in range(quarter):
+        near_p, far_p = xp[p], xp[p + quarter]
+        xh[p] = jnp.where(part < 4, near_p, pltpu.roll(far_p, 4, 1))
+        xw[p] = jnp.where(part >= 4, near_p, pltpu.roll(far_p, lanes - 4, 1))
     pl.semaphore_wait(barrier, len(near))
 
     def send(i, src, dst, peer):
@@ -89,6 +90,10 @@
         return copy
 
     mid_y = pl.ds(8, ys)
+    rows_x = [
+        send(0, xh, xl, away("gx", 1)),
+        send(1, xw, xr, away("gx", -1)),
+    ]
     rows_y = [
         send(2, yph, yrh, away("gy", 1)),
         send(3, ypl, yrl, away("gy", -1)),
@@ -98,16 +103,6 @@
         send(5, xe.at[pl.ds(4, 4), mid_y, :], xe.at[pl.ds(zs + 4, 4), mid_y, :], away("gz", -1)),
     ]
     tell(known.at[0], near)
-    lax.fori_loop(0, zs // 8, pack_x, 0)
-    quarter = zs // 4
-    for p in range(quarter):
-        near_p, far_p = xp[p], xp[p + quarter]
-        xh[p] = jnp.where(part < 4, near_p, pltpu.roll(far_p, 4, 1))
-        xw[p] = jnp.where(part >= 4, near_p, pltpu.roll(far_p, lanes - 4, 1))
-    rows_x = [
-        send(0, xh, xl, away("gx", 1)),
-        send(1, xw, xr, away("gx", -1)),
-    ]
 
     def unpack_y(i, carry):
         z = 4 + 2 * i

time: 38.1 us -> 38.1 us (level)
  no operation moved by 1% of the time
where the time goes in v5:
time: 38.1 us; the launch traced here: 38 us
  Pallas kernels  36 us (94%)
  between operations  1.94 us (5%)
    pallas_call x1, Pallas kernels, on_device(): pl.pallas_call(lambda *refs: kernel(nx, ny, nz, cells, *refs), name='fiel...  34.9 us
    pallas_call x1, Pallas kernels, on_device(): pl.pallas_call(finish, name='finish', out_shape=tuple((jax.ShapeDtypeStru...  1 us

profile of v5, /device:TPU:1, one launch (start us, length us, event | category | flops | bytes accessed | tf_op | source)
XLA Modules:
  0.0 38.0 jit_solution(1449008009929987551)
XLA Ops:
  1.9 0.1 concatenate.6.refs_0_
  2.0 34.9 %field.1 = (f32[32,64,128]{2,1,0:T(8,128)S(1)}, f32[2,128]{1,0:T(2,128)S(1)}, f32[1,4]{1,0:T(1,128)S(1)}) custom-call(f32[2,128]{1,0:T(2,128)S(1)} %concatenate.6.refs_0_, f32[32,64,128]{2,1,0:T(8,128)} %refs_1_.1), custom_call_target="tpu_custom_call" | custom-call | tf_op jit(solution)/shard_map/field/pallas_call | solution.py:319
  37.0 1.0 %finish.1 = (f32[32,64,128]{2,1,0:T(8,128)}, f32[2,128]{1,0:T(2,128)}, f32[1,4]{1,0:T(1,128)}) custom-call(f32[32,64,128]{2,1,0:T(8,128)S(1)} %get-tuple-element.9.mag, f32[2,128]{1,0:T(2,128)S(1)} %get-tuple-element.10.hist, f32[1,4]{1,0:T(1,128)S(1)} %get-tuple-element.11.stat), custom_call_target="tpu_custom_call" | custom-call | tf_op jit(solution)/shard_map/finish/pallas_call | solution.py:341
  (1 shorter events, 0.0 us)
